TPU v7x, 32 devices: a whole 2x2x4 slice. The times are simulated.
32 devices in a mesh: row: 8 (over y, x, core), col: 4 (over z).
Axes of the slice: x: 2, y: 2, z: 4, core: 2. Of those that a mesh axis runs over, the one named last changes fastest.
Arguments:
- vectors: float32 [16384, 16384], P('row', 'col'), may hold values from -0.046875 to 0.046875
- basis: float32 [16384, 2048], P('col', 'row'), may hold values from -9 to 9
- block_units: int32 [8], replicated, may hold values from 1 to 40, 64 in all
Outputs:
- assembled: float32 [16384, 2048], P('row', 'col')
Inputs may be any that keep to these rules, and one draw needn't show every extreme that they name: `block_units`: the block sizes are whole numbers of units that sum to 64; the largest is exactly the maximum.
All inputs are finite; a program needn't handle non-finite values.
Results may differ from a plain program's by a relative error of at most 0.00007.
Values sent between devices are 32-bit elements; how exact they have to be, the bound alone decides.
A program may use at most 192 MiB of HBM per device.

v0:
```python
import jax
import jax.numpy as jnp
from jax import lax
from jax.sharding import PartitionSpec as P

UNIT = 256
START = 7168
LANES = 128


def block_ids(positions, block_units):
    ends = jnp.cumsum(block_units) * UNIT
    return jnp.sum((positions[:, None] >= ends[None, :-1]).astype(jnp.int32), axis=1)


def shards(vectors, basis, block_units):
    inner, width = basis.shape
    row_block = block_ids(
        lax.axis_index("col") * inner + jnp.arange(inner, dtype=jnp.int32), block_units
    )
    slab_block = block_ids(
        START + lax.axis_index("row") * width + jnp.arange(width, dtype=jnp.int32), block_units
    )
    masked = jnp.where(row_block[:, None] == slab_block[None, :], basis, jnp.float32(0.0))
    rows, cols = (lax.axis_size("row"), lax.axis_size("col"))
    step = LANES if width % LANES == 0 and rows % cols == 0 else width
    pieces = [
        lax.all_gather(masked[:, at : at + step], "row", axis=1, tiled=True)
        for at in range(0, width, step)
    ]
    sums = []
    for piece in pieces:
        part = jnp.dot(
            vectors, piece, precision=lax.Precision.HIGH, preferred_element_type=jnp.float32
        )
        sums.append(lax.psum_scatter(part, "col", scatter_dimension=1, tiled=True))
    groups = sums[0].shape[1] // step
    return jnp.concatenate(
        [one[:, g * step : (g + 1) * step] for g in range(groups) for one in sums], axis=1
    )


def solution(mesh):
    in_specs = (P("row", "col"), P("col", "row"), P())
    out_specs = P("row", "col")
    return jax.shard_map(shards, mesh=mesh, in_specs=in_specs, out_specs=out_specs, check_vma=False)
```

profile of v0, /device:TPU:0, one launch (start us, length us, event | category | flops | bytes accessed | tf_op | source)
XLA Modules:
  0.0 529.0 jit_solution(5976717857978838351)
XLA Ops:
  6.5 0.0 all-gather.3.cloned.1.call-start
  6.5 0.8 reduce-window.9
  7.4 0.1 convert_reduce_fusion.1
  7.5 0.1 convert_reduce_fusion
  7.6 3.9 compare_select_fusion
  11.5 2.3 fusion
  13.8 0.0 all-gather.3.cloned.1.call-update
  13.9 0.0 all-gather.5.cloned.1.call-start
  13.9 0.7 all-gather.5.cloned.1.call-update
  14.6 0.0 reduce-scatter.3.cloned.1.call-start
  14.7 95.1 %all-gather.3.cloned.1.call-done = f32[4096,1024]{1,0:T(8,128)} async-done(((f32[4096,128]{1,0:T(8,128)}), f32[4096,1024]{1,0:T(8,128)}) %all-gather.3.cloned.1.call-update) | async-done | bytes 16777232 | tf_op jit(solution)/shard_map/all_gather | solution.py:28
  109.8 111.0 %convolution_bitcast_fusion.1 = f32[2048,1024]{0,1:T(8,128)} fusion(f32[4096,1024]{1,0:T(8,128)} %all-gather.3.cloned.1.call-done, f32[2048,4096]{1,0:T(8,128)} %param.3), kind=kOutput, calls=%fused_computation.1 | convolution fusion | flops 51539607552 | bytes 58720256 | tf_op jit(solution)/shard_map/dot_general | solution.py:33
  220.7 0.0 reduce-scatter.3.cloned.1.call-update
  220.8 0.0 reduce-scatter.5.cloned.1.call-start
  220.8 0.0 all-gather.5.cloned.1.call-done
  220.8 111.1 %convolution_bitcast_fusion = f32[2048,1024]{0,1:T(8,128)} fusion(f32[4096,1024]{1,0:T(8,128)} %all-gather.5.cloned.1.call-done, f32[2048,4096]{1,0:T(8,128)} %param.3), kind=kOutput, calls=%fused_computation | convolution fusion | flops 51539607552 | bytes 58720256 | tf_op jit(solution)/shard_map/dot_general | solution.py:33
  332.0 0.0 reduce-scatter.5.cloned.1.call-update
  332.0 33.5 %reduce-scatter.3.cloned.1.call-done = f32[2048,256]{0,1:T(8,128)} async-done(((f32[2048,1024]{0,1:T(8,128)}), f32[2048,256]{0,1:T(8,128)}) %reduce-scatter.3.cloned.1.call-update) | async-done | bytes 2097168 | tf_op jit(solution)/shard_map/reduce_scatter | solution.py:36
  365.5 1.7 fusion.1
  367.2 145.8 %reduce-scatter.5.cloned.1.call-done = f32[2048,256]{0,1:T(8,128)} async-done(((f32[2048,1024]{0,1:T(8,128)}), f32[2048,256]{0,1:T(8,128)}) %reduce-scatter.5.cloned.1.call-update) | async-done | bytes 2097168 | tf_op jit(solution)/shard_map/reduce_scatter | solution.py:36
  513.0 1.8 fusion.2
  514.8 2.3 pad_maximum_fusion
  517.1 5.3 %copy.5 = f32[2048,512]{1,0:T(8,128)} copy(f32[2048,512]{0,1:T(8,128)} %pad_maximum_fusion) | data formatting | bytes 8388608 | tf_op jit(solution)/shard_map/concatenate | solution.py:38
  (4 shorter events, 0.0 us)
Async XLA Ops:
  6.5 103.2 %all-gather.3.cloned.1.call-start = ((), (), s32[]{:S(2)}) async-start(), calls=%async_computation.2 | async-start | bytes 18874368 | tf_op jit(solution)/shard_map/all_gather | solution.py:28
  13.9 207.0 %all-gather.5.cloned.1.call-start = ((), (), s32[]{:S(2)}) async-start(), calls=%async_computation.4 | async-start | bytes 18874368 | tf_op jit(solution)/shard_map/all_gather | solution.py:28
  14.6 350.9 %reduce-scatter.3.cloned.1.call-start = ((), (), s32[]{:S(2)}) async-start(), calls=%async_computation.3 | async-start | bytes 10485760 | tf_op jit(solution)/shard_map/reduce_scatter | solution.py:36
  220.8 292.2 %reduce-scatter.5.cloned.1.call-start = ((), (), s32[]{:S(2)}) async-start(), calls=%async_computation.5 | async-start | bytes 10485760 | tf_op jit(solution)/shard_map/reduce_scatter | solution.py:36
Sparse Core Ops, SparseCore 0:
  14.0 95.7 all-gather.2
  111.6 93.0 all-gather.4
  220.9 144.6 reduce-scatter.2
  367.7 145.2 reduce-scatter.4
where the time goes:
time: 529 us
  waiting for transfers between devices  275 us (52%)
  matrix products  222 us (42%)
  between operations  13.2 us (2%)
  local copies, waits for them, and re-layouts  11.1 us (2%)
  other arithmetic  7.3 us (1%)
    dot_general x2, matrix products, shards(): jnp.dot(vectors, piece, precision=lax.Precision.HIGH, preferred_element_t...  222 us
    reduce_scatter x2, waiting for transfers between devices, shards(): sums.append(lax.psum_scatter(part, 'col', scatter_dimension=1, tiled=True))  179 us
    all_gather x2, waiting for transfers between devices, shards(): lax.all_gather(masked[:, at:at + step], 'row', axis=1, tiled=True)  95.1 us
  transfers between devices with their start and end apart: 4, of which 3 were waited for; matrix products, arithmetic and copies ran while one was open for 42% of the time, Pallas kernels for 0%

commit v1 on v0

--- a/solution.py
+++ b/solution.py
@@ -24,10 +24,8 @@
     masked = jnp.where(row_block[:, None] == slab_block[None, :], basis, jnp.float32(0.0))
     rows, cols = (lax.axis_size("row"), lax.axis_size("col"))
     step = LANES if width % LANES == 0 and rows % cols == 0 else width
-    pieces = [
-        lax.all_gather(masked[:, at : at + step], "row", axis=1, tiled=True)
-        for at in range(0, width, step)
-    ]
+    node_lead = lambda z: jnp.concatenate(lax.all_gather(z, axis_name="row"), axis=1)
+    pieces = [node_lead(masked[:, at : at + step]) for at in range(0, width, step)]
     sums = []
     for piece in pieces:
         part = jnp.dot(

time: 529 us -> 509 us (0.962)
  matrix products: 222 us -> 119 us
  waiting for transfers between devices: 275 us -> 322 us
  local copies, waits for them, and re-layouts: 11.1 us -> 46.6 us
    dot_general x2, matrix products: 222 us -> 119 us  [shards(): jnp.dot(vectors, piece, precision=lax.Precision.HIGH, preferred_element_t...]
    reduce_scatter x2, waiting for transfers between devices: 179 us -> 215 us  [shards(): sums.append(lax.psum_scatter(part, 'col', scatter_dimension=1, tiled=True))]
    reshape x0 -> x2, local copies, waits for them, and re-layouts: none -> 35.5 us  [shards(): jnp.concatenate(lax.all_gather(z, axis_name='row'), axis=1)]
    all_gather x2, waiting for transfers between devices: 95.1 us -> 106 us  [shards(): lax.all_gather(z, axis_name='row')]
  transfers between devices with their start and end apart: 4 -> 4, of which waited for: 3 -> 4; matrix products, arithmetic and copies ran while one was open for 42% -> 31% of each run, Pallas kernels for 0% -> 0%
where the time goes in v1:
time: 509 us
  waiting for transfers between devices  322 us (63%)
  matrix products  119 us (23%)
  local copies, waits for them, and re-layouts  46.6 us (9%)
  between operations  13.2 us (3%)
  other arithmetic  7.3 us (1%)
    reduce_scatter x2, waiting for transfers between devices, shards(): sums.append(lax.psum_scatter(part, 'col', scatter_dimension=1, tiled=True))  215 us
    dot_general x2, matrix products, shards(): jnp.dot(vectors, piece, precision=lax.Precision.HIGH, preferred_element_t...  119 us
    all_gather x2, waiting for transfers between devices, shards(): lax.all_gather(z, axis_name='row')  106 us
    reshape x2, local copies, waits for them, and re-layouts, shards(): jnp.concatenate(lax.all_gather(z, axis_name='row'), axis=1)  35.5 us
  transfers between devices with their start and end apart: 4, of which 4 were waited for; matrix products, arithmetic and copies ran while one was open for 31% of the time, Pallas kernels for 0%

profile of v1, /device:TPU:0, one launch (start us, length us, event | category | flops | bytes accessed | tf_op | source)
XLA Modules:
  0.0 508.6 jit_solution(12102702186903524368)
XLA Ops:
  6.5 0.0 all-gather.5.cloned.1.call-start
  6.5 0.8 reduce-window.9
  7.4 0.1 convert_reduce_fusion.1
  7.5 0.1 convert_reduce_fusion
  7.6 3.9 compare_select_fusion
  11.5 2.3 fusion
  13.8 0.0 all-gather.5.cloned.1.call-update
  13.8 0.0 all-gather.7.cloned.1.call-start
  13.9 0.7 all-gather.7.cloned.1.call-update
  14.6 0.0 reduce-scatter.3.cloned.1.call-start
  14.6 91.8 %all-gather.5.cloned.1.call-done = f32[32768,128]{1,0:T(8,128)} async-done(((f32[4096,128]{1,0:T(8,128)}), f32[32768,128]{1,0:T(8,128)}) %all-gather.5.cloned.1.call-update) | async-done | bytes 16777232 | tf_op jit(solution)/shard_map/all_gather | solution.py:27
  106.5 17.9 %copy.9 = f32[4096,8,128]{0,2,1:T(8,128)} copy(f32[4096,8,128]{2,0,1:T(8,128)} %bitcast.20) | data formatting | bytes 33554432 | tf_op jit(solution)/shard_map/reshape | solution.py:27
  124.4 59.7 %convolution_bitcast_fusion.1 = f32[2048,1024]{0,1:T(8,128)} fusion(f32[4096,1024]{0,1:T(8,128)} %bitcast.21, f32[2048,4096]{1,0:T(8,128)} %param.3), kind=kOutput, calls=%fused_computation.1 | convolution fusion | flops 51539607552 | bytes 58720256 | tf_op jit(solution)/shard_map/dot_general | solution.py:31
  184.1 0.0 reduce-scatter.3.cloned.1.call-update
  184.1 0.2 reduce-scatter.5.cloned.1.call-start
  184.3 13.8 %all-gather.7.cloned.1.call-done = f32[32768,128]{1,0:T(8,128)} async-done(((f32[4096,128]{1,0:T(8,128)}), f32[32768,128]{1,0:T(8,128)}) %all-gather.7.cloned.1.call-update) | async-done | bytes 16777232 | tf_op jit(solution)/shard_map/all_gather | solution.py:27
  198.1 17.6 %copy.10 = f32[4096,8,128]{0,2,1:T(8,128)} copy(f32[4096,8,128]{2,0,1:T(8,128)} %bitcast.19) | data formatting | bytes 33554432 | tf_op jit(solution)/shard_map/reshape | solution.py:27
  215.7 59.7 %convolution_bitcast_fusion = f32[2048,1024]{0,1:T(8,128)} fusion(f32[4096,1024]{0,1:T(8,128)} %bitcast.22, f32[2048,4096]{1,0:T(8,128)} %param.3), kind=kOutput, calls=%fused_computation | convolution fusion | flops 51539607552 | bytes 58720256 | tf_op jit(solution)/shard_map/dot_general | solution.py:31
  275.4 0.0 reduce-scatter.5.cloned.1.call-update
  275.4 69.7 %reduce-scatter.3.cloned.1.call-done = f32[2048,256]{0,1:T(8,128)} async-done(((f32[2048,1024]{0,1:T(8,128)}), f32[2048,256]{0,1:T(8,128)}) %reduce-scatter.3.cloned.1.call-update) | async-done | bytes 2097168 | tf_op jit(solution)/shard_map/reduce_scatter | solution.py:34
  345.1 1.7 fusion.1
  346.8 145.8 %reduce-scatter.5.cloned.1.call-done = f32[2048,256]{0,1:T(8,128)} async-done(((f32[2048,1024]{0,1:T(8,128)}), f32[2048,256]{0,1:T(8,128)}) %reduce-scatter.5.cloned.1.call-update) | async-done | bytes 2097168 | tf_op jit(solution)/shard_map/reduce_scatter | solution.py:34
  492.6 1.8 fusion.2
  494.3 2.3 pad_maximum_fusion
  496.7 5.3 %copy.11 = f32[2048,512]{1,0:T(8,128)} copy(f32[2048,512]{0,1:T(8,128)} %pad_maximum_fusion) | data formatting | bytes 8388608 | tf_op jit(solution)/shard_map/concatenate | solution.py:36
  (4 shorter events, 0.0 us)
Async XLA Ops:
  6.5 99.9 %all-gather.5.cloned.1.call-start = ((), (), s32[]{:S(2)}) async-start(), calls=%async_computation.4 | async-start | bytes 18874368 | tf_op jit(solution)/shard_map/all_gather | solution.py:27
  13.8 184.3 %all-gather.7.cloned.1.call-start = ((), (), s32[]{:S(2)}) async-start(), calls=%async_computation.5 | async-start | bytes 18874368 | tf_op jit(solution)/shard_map/all_gather | solution.py:27
  14.6 330.5 %reduce-scatter.3.cloned.1.call-start = ((), (), s32[]{:S(2)}) async-start(), calls=%async_computation.2 | async-start | bytes 10485760 | tf_op jit(solution)/shard_map/reduce_scatter | solution.py:34
  184.1 308.5 %reduce-scatter.5.cloned.1.call-start = ((), (), s32[]{:S(2)}) async-start(), calls=%async_computation.3 | async-start | bytes 10485760 | tf_op jit(solution)/shard_map/reduce_scatter | solution.py:34
Sparse Core Ops, SparseCore 0:
  14.0 92.4 all-gather.4
  108.3 89.7 all-gather.6
  200.5 144.6 reduce-scatter.2
  347.3 145.2 reduce-scatter.4
